TPU v7x, 32 devices: a whole 2x2x4 slice. The times are simulated.
32 devices in a mesh: group: 2 (over x), tensor: 16 (over z, y, core).
Axes of the slice: x: 2, y: 2, z: 4, core: 2. Of those that a mesh axis runs over, the one named last changes fastest.
Arguments:
- z_star: bfloat16 [64, 5120], P(('group', 'tensor')), parts along dimension 0, may hold values from -6 to 6
- grad_out: float32 [64, 5120], P(('group', 'tensor')), parts along dimension 0, may hold values from -30 to 30
- w_gate: bfloat16 [10240, 13824], P('group', 'tensor'), parts along dimension 0, may hold values from -0.078125 to 0.078125
- w_up: bfloat16 [10240, 13824], P('group', 'tensor'), parts along dimension 0, may hold values from -0.078125 to 0.078125
- w_down: bfloat16 [27648, 5120], P(('group', 'tensor')), parts along dimension 0, may hold values from -0.0546875 to 0.0546875
- norm_gain: float32 [10240], P('group'), parts along dimension 0, may hold values from 0.5 to 1.5
- mix_rate: float32 [10240], P('group'), parts along dimension 0, may hold values from 0.3 to 1
Outputs:
- adjoint: float32 [64, 5120], P(('group', 'tensor')), parts along dimension 0
- grad_gate: bfloat16 [10240, 13824], P('group', 'tensor'), parts along dimension 0
- grad_up: bfloat16 [10240, 13824], P('group', 'tensor'), parts along dimension 0
- grad_down: bfloat16 [27648, 5120], P(('group', 'tensor')), parts along dimension 0
There are 2 independent parts, one for each index of `group`. A program takes and returns all parts, laid end to end along the dimension named above; each array names one. Nothing has to cross between parts.
All inputs are finite; a program needn't handle non-finite values.
Results may differ from a plain program's by a relative error of at most 0.014.
Values may be sent and summed in bfloat16 or wider, within the bound.
No kernel may reach another device: no remote copies, remote signals or barrier semaphores. Data moves between devices by JAX's collectives and lax.ppermute only.
A program may use at most 128 MiB of HBM per device.

v0:
```python
import jax
import jax.numpy as jnp
from jax import lax
from jax.sharding import PartitionSpec as P


def contract(left, right, left_dim, right_dim):
    return lax.dot_general(
        left, right, (((left_dim,), (right_dim,)), ((), ())), preferred_element_type=jnp.float32
    )


def normalize(z_rows, norm_gain):
    values = z_rows.astype(jnp.float32)
    root_mean = jnp.sqrt(jnp.mean(values * values, axis=-1, keepdims=True) + 1e-06)
    unit_rows = values / root_mean
    normed = (unit_rows * norm_gain).astype(jnp.bfloat16)
    return (root_mean, unit_rows, normed)


def norm_back(normed_grad, norm_gain, unit_rows, root_mean):
    scaled = norm_gain * normed_grad
    return (scaled - unit_rows * jnp.mean(scaled * unit_rows, axis=-1, keepdims=True)) / root_mean


def body(z_star, grad_out, w_gate, w_up, w_down, norm_gain, mix_rate):
    local_rows = z_star.shape[0]
    z_full = lax.all_gather(z_star, "tensor", axis=0, tiled=True)
    root_mean, unit_rows, normed = normalize(z_full, norm_gain)
    gate_pre = contract(normed, w_gate, 1, 0)
    lifted = contract(normed, w_up, 1, 0)
    sigma = jax.nn.sigmoid(gate_pre)
    gated = gate_pre * sigma
    slope = sigma * (1.0 + gate_pre * (1.0 - sigma))
    hidden = (gated * lifted).astype(jnp.bfloat16)

    def branch_rows(state_half):
        hidden_grad = contract(state_half, w_down, 1, 1)
        gate_grad = (hidden_grad * lifted * slope).astype(jnp.bfloat16)
        lift_grad = (hidden_grad * gated).astype(jnp.bfloat16)
        return (gate_grad, lift_grad)

    cotangent = lax.all_gather(grad_out.astype(jnp.bfloat16), "tensor", axis=0, tiled=True).astype(
        grad_out.dtype
    )

    def jacobian(state):
        gate_grad, lift_grad = branch_rows(state.astype(jnp.bfloat16))
        partial_sum = contract(gate_grad, w_gate, 1, 1) + contract(lift_grad, w_up, 1, 1)
        normed_grad = lax.psum(partial_sum, "tensor")
        return norm_back(normed_grad, norm_gain, unit_rows, root_mean)

    resid_zero = jacobian(cotangent)
    state_one = cotangent + mix_rate * resid_zero
    resid_one = cotangent + jacobian(state_one) - state_one
    resid_diff = resid_one - resid_zero
    blend = jnp.sum(resid_one * resid_diff) / (jnp.sum(resid_diff * resid_diff) + 1e-06)
    adjoint = (
        state_one - blend * (state_one - cotangent) + mix_rate * (resid_one - blend * resid_diff)
    )
    adjoint_half = adjoint.astype(jnp.bfloat16)
    gate_grad, lift_grad = branch_rows(adjoint_half)
    grad_gate = contract(normed, gate_grad, 0, 0)
    grad_up = contract(normed, lift_grad, 0, 0)
    grad_down = contract(hidden, adjoint_half, 0, 0)
    adjoint_own = lax.dynamic_slice_in_dim(
        adjoint, lax.axis_index("tensor") * local_rows, local_rows, 0
    )
    return (
        adjoint_own,
        grad_gate.astype(jnp.bfloat16),
        grad_up.astype(jnp.bfloat16),
        grad_down.astype(jnp.bfloat16),
    )


def solution(mesh):
    placed = (
        P(("group", "tensor"), None),
        P(("group", "tensor"), None),
        P("group", "tensor"),
        P("group", "tensor"),
        P(("group", "tensor"), None),
        P("group"),
        P("group"),
    )
    return jax.shard_map(
        body,
        mesh=mesh,
        in_specs=placed,
        out_specs=(
            P(("group", "tensor"), None),
            P("group", "tensor"),
            P("group", "tensor"),
            P(("group", "tensor"), None),
        ),
        check_vma=False,
    )
```

profile of v0, /device:TPU:0, one launch (start us, length us, event | category | flops | bytes accessed | tf_op | source)
XLA Modules:
  0.0 303.7 jit_solution(8700253727963858324)
XLA Ops:
  7.2 0.0 all-reduce.3.cloned.1.call-start
  7.2 0.8 convert_bitcast_fusion
  8.0 24.0 %all-gather = bf16[16,2,5120]{2,1,0:T(2,128)(2,1)S(1)} all-gather(bf16[1,2,5120]{2,1,0:T(2,128)(2,1)S(1)} %convert_bitcast_fusion), channel_id=1, replica_groups=mesh['group'=2,'tensor'=16] {'tensor'}, dimensions={0}, use_global_device_ids=true | all-gather | bytes 348160 | tf_op jit(solution)/shard_map/all_gather | solution.py:43
  32.0 0.1 reshape.27
  32.2 18.6 %all-gather.1 = bf16[16,2,5120]{2,1,0:T(2,128)(2,1)S(1)} all-gather(bf16[1,2,5120]{2,1,0:T(2,128)(2,1)} %bitcast.21), channel_id=1, replica_groups=mesh['group'=2,'tensor'=16] {'tensor'}, dimensions={0}, use_global_device_ids=true | all-gather | bytes 348160 | tf_op jit(solution)/shard_map/all_gather | solution.py:28
  50.7 0.1 reshape.30
  50.8 0.0 copy-start
  50.8 0.2 multiply_reduce_fusion.4
  51.0 1.0 multiply_convert_fusion
  52.0 0.0 copy-start.1
  52.1 6.6 %fusion.21 = f32[32,864]{1,0:T(8,128)S(1)} fusion(bf16[32,5120]{1,0:T(8,128)(2,1)S(1)} %multiply_convert_fusion, bf16[5120,864]{0,1:T(8,128)(2,1)} %param.9), kind=kOutput, calls=%fused_computation.45 | convolution fusion | flops 283115520 | bytes 9285632 | tf_op jit(solution)/shard_map/dot_general | solution.py:8
  58.7 0.0 copy-done
  58.7 0.0 slice-start
  58.7 0.0 slice-start.1
  58.8 2.7 fusion.20
  61.4 0.0 copy-done.1
  61.4 0.0 slice-start.2
  61.4 2.7 fusion.19
  64.1 0.0 slice-done
  64.1 0.0 slice-done.1
  64.1 0.0 slice-done.2
  64.2 1.6 fusion.12
  65.8 0.0 copy-start.2
  65.8 0.0 copy-start.3
  65.8 2.5 convolution_add_fusion.1
  68.3 0.0 all-reduce.3.cloned.1.call-update
  68.3 0.2 all-reduce.5.cloned.1.call-start
  68.5 90.0 %all-reduce.3.cloned.1.call-done = f32[32,5120]{1,0:T(8,128)} async-done(((f32[32,5120]{1,0:T(8,128)}), f32[32,5120]{1,0:T(8,128)}) %all-reduce.3.cloned.1.call-update) | async-done | bytes 655376 | tf_op jit(solution)/shard_map/psum | solution.py:50
  158.5 0.0 copy-done.2
  158.5 1.3 multiply_reduce_fusion.3
  159.8 1.3 subtract_divide_fusion
  161.1 0.0 copy-done.3
  161.1 0.0 slice-start.3
  161.1 0.0 slice-start.4
  161.1 6.3 %fusion.5 = f32[32,864]{1,0:T(8,128)S(1)} fusion(bf16[864,5120]{1,0:T(8,128)(2,1)} %param.11, f32[32,5120]{1,0:T(8,128)S(1)} %subtract_divide_fusion, bf16[32,5120]{1,0:T(8,128)(2,1)S(1)} %reshape.27, f32[5120]{0:T(1024)S(1)} %copy-done.3), kind=kOutput, calls=%fused_computation.20 | convolution fusion | flops 283770880 | bytes 9961472 | tf_op jit(solution)/shard_map/dot_general | solution.py:8
  167.5 0.0 slice-start.5
  167.5 5.3 %fusion.13 = f32[32,5120]{1,0:T(8,128)S(1)} fusion(bf16[5120,864]{0,1:T(8,128)(2,1)} %param.9, f32[32,864]{1,0:T(8,128)S(1)} %fusion.5, f32[32,864]{1,0:T(8,128)S(1)} %fusion.20, f32[32,864]{1,0:T(8,128)S(1)} %fusion.21), kind=kOutput, calls=%fused_computation.37 | convolution fusion | flops 283392000 | bytes 9834496 | tf_op jit(solution)/shard_map/dot_general | solution.py:8
  172.8 0.0 slice-done.3
  172.8 0.0 slice-done.4
  172.8 0.0 slice-done.5
  172.8 2.5 convolution_add_fusion
  175.3 0.0 all-reduce.5.cloned.1.call-update
  175.3 91.6 %all-reduce.5.cloned.1.call-done = f32[32,5120]{1,0:T(8,128)} async-done(((f32[32,5120]{1,0:T(8,128)}), f32[32,5120]{1,0:T(8,128)}) %all-reduce.5.cloned.1.call-update) | async-done | bytes 655376 | tf_op jit(solution)/shard_map/psum | solution.py:50
  266.9 1.3 multiply_reduce_fusion.2
  268.2 2.1 multiply_reduce_fusion
  271.6 0.2 fusion.3
  271.8 6.1 %fusion.9 = f32[32,864]{1,0:T(8,128)S(1)} fusion(bf16[864,5120]{1,0:T(8,128)(2,1)} %param.11, f32[32,5120]{1,0:T(8,128)S(1)} %fusion.3), kind=kOutput, calls=%fused_computation.24 | convolution fusion | flops 283279360 | bytes 9613312 | tf_op jit(solution)/shard_map/dot_general | solution.py:8
  278.0 6.1 %convolution_convert_fusion = bf16[864,5120]{1,0:T(8,128)(2,1)} fusion(f32[32,5120]{1,0:T(8,128)S(1)} %fusion.3, f32[32,864]{1,0:T(8,128)S(1)} %fusion.20, f32[32,864]{1,0:T(8,128)S(1)} %fusion.21), kind=kOutput, calls=%fused_computation | convolution fusion | flops 287868928 | bytes 9723904 | tf_op jit(solution)/shard_map/dot_general | solution.py:8
  284.1 6.1 %convolution_convert_fusion.2 = bf16[5120,864]{0,1:T(8,128)(2,1)} fusion(bf16[32,5120]{1,0:T(8,128)(2,1)S(1)} %multiply_convert_fusion, f32[32,864]{1,0:T(8,128)S(1)} %fusion.9, f32[32,864]{1,0:T(8,128)S(1)} %fusion.20, f32[32,864]{1,0:T(8,128)S(1)} %fusion.21), kind=kOutput, calls=%fused_computation.2 | convolution fusion | flops 287815680 | bytes 9506816 | tf_op jit(solution)/shard_map/dot_general | solution.py:8
  290.1 6.1 %convolution_convert_fusion.1 = bf16[5120,864]{0,1:T(8,128)(2,1)} fusion(bf16[32,5120]{1,0:T(8,128)(2,1)S(1)} %multiply_convert_fusion, f32[32,864]{1,0:T(8,128)S(1)} %fusion.9, f32[32,864]{1,0:T(8,128)S(1)} %fusion.21), kind=kOutput, calls=%fused_computation.1 | convolution fusion | flops 287705088 | bytes 9396224 | tf_op jit(solution)/shard_map/dot_general | solution.py:8
  296.2 0.6 constant_dynamic-slice_fusion
  (5 shorter events, 0.0 us)
Async XLA Ops:
  7.2 151.3 %all-reduce.3.cloned.1.call-start = ((), (), s32[]{:S(2)}) async-start(), calls=%async_computation | async-start | bytes 1310720 | tf_op jit(solution)/shard_map/psum | solution.py:50
  50.8 7.9 %copy-start = (bf16[5120,864]{0,1:T(8,128)(2,1)S(1)}, bf16[5120,864]{0,1:T(8,128)(2,1)}, u32[]{:S(2)}) copy-start(bf16[5120,864]{0,1:T(8,128)(2,1)} %param.10) | copy-start | bytes 26542084
  52.0 9.4 %copy-start.1 = (bf16[864,5120]{1,0:T(8,128)(2,1)S(1)}, bf16[864,5120]{1,0:T(8,128)(2,1)}, u32[]{:S(2)}) copy-start(bf16[864,5120]{1,0:T(8,128)(2,1)} %param.11) | copy-start | bytes 26542084
  58.7 5.4 %slice-start = ((s8[8847360]{0:T(1024)(128)(4,1)}), s8[4194304]{0:T(1024)(128)(4,1)S(1)}, s32[]{:S(2)}) async-start(s8[8847360]{0:T(1024)(128)(4,1)} %bitcast.17), calls=%async_computation.2 | async-start | bytes 8388608
  58.7 5.4 %slice-start.1 = ((s8[8847360]{0:T(1024)(128)(4,1)}), s8[4194304]{0:T(1024)(128)(4,1)S(1)}, s32[]{:S(2)}) async-start(s8[8847360]{0:T(1024)(128)(4,1)} %bitcast.17), calls=%async_computation.3 | async-start | bytes 8388608
  61.4 2.7 slice-start.2
  65.8 92.7 %copy-start.2 = (f32[5120]{0:T(1024)S(1)}, f32[5120]{0:T(1024)}, u32[]{:S(2)}) copy-start(f32[5120]{0:T(1024)} %param.12) | copy-start | bytes 61444
  65.8 95.3 %copy-start.3 = (f32[5120]{0:T(1024)S(1)}, f32[5120]{0:T(1024)}, u32[]{:S(2)}) copy-start(f32[5120]{0:T(1024)} %param.13) | copy-start | bytes 61444
  68.3 198.6 %all-reduce.5.cloned.1.call-start = ((), (), s32[]{:S(2)}) async-start(), calls=%async_computation.1 | async-start | bytes 1310720 | tf_op jit(solution)/shard_map/psum | solution.py:50
  161.1 11.6 %slice-start.3 = ((s8[8847360]{0:T(1024)(128)(4,1)}), s8[4194304]{0:T(1024)(128)(4,1)S(1)}, s32[]{:S(2)}) async-start(s8[8847360]{0:T(1024)(128)(4,1)} %bitcast.19), calls=%async_computation.5 | async-start | bytes 8388608
  161.1 11.6 %slice-start.4 = ((s8[8847360]{0:T(1024)(128)(4,1)}), s8[458752]{0:T(1024)(128)(4,1)S(1)}, s32[]{:S(2)}) async-start(s8[8847360]{0:T(1024)(128)(4,1)} %bitcast.19), calls=%async_computation.6 | async-start | bytes 917504
  167.5 5.3 %slice-start.5 = ((s8[8847360]{0:T(1024)(128)(4,1)}), s8[4194304]{0:T(1024)(128)(4,1)S(1)}, s32[]{:S(2)}) async-start(s8[8847360]{0:T(1024)(128)(4,1)} %bitcast.19), calls=%async_computation.7 | async-start | bytes 8388608
Sparse Core Ops, SparseCore 0:
  68.4 90.0 all-reduce.2
  175.4 91.4 all-reduce.4
where the time goes:
time: 304 us
  waiting for transfers between devices  182 us (60%)
  matrix products  54.4 us (18%)
  blocking collectives  42.6 us (14%)
  between operations  15.5 us (5%)
  other arithmetic  8.24 us (3%)
    psum x2, waiting for transfers between devices, jacobian(): normed_grad = lax.psum(partial_sum, 'tensor')  182 us
    dot_general x12, matrix products, contract(): lax.dot_general(left, right, (((left_dim,), (right_dim,)), ((), ())), pre...  54.4 us
    all_gather x1, blocking collectives, body(): lax.all_gather(grad_out.astype(jnp.bfloat16), 'tensor', axis=0, tiled=True)  24 us
    all_gather x1, blocking collectives, body(): z_full = lax.all_gather(z_star, 'tensor', axis=0, tiled=True)  18.6 us
  transfers between devices with their start and end apart: 2, of which 2 were waited for; matrix products, arithmetic and copies ran while one was open for 0% of the time, Pallas kernels for 0%

commit v1 on v0

--- a/solution.py
+++ b/solution.py
@@ -2,6 +2,22 @@
 import jax.numpy as jnp
 from jax import lax
 from jax.sharding import PartitionSpec as P
+
+
+def gather_around(x, axis, dim):
+    ways, here, step = (lax.axis_size(axis), lax.axis_index(axis), x.shape[dim])
+    lengths = [n * ways if d == dim else n for d, n in enumerate(x.shape)]
+    full = lax.dynamic_update_slice_in_dim(jnp.zeros(lengths, x.dtype), x, here * step, axis=dim)
+    going_up = going_down = x
+    for far in range(1, ways // 2 + 1):
+        going_up = lax.ppermute(going_up, axis, [(d, (d + 1) % ways) for d in range(ways)])
+        full = lax.dynamic_update_slice_in_dim(full, going_up, (here - far) % ways * step, axis=dim)
+        if 2 * far < ways:
+            going_down = lax.ppermute(going_down, axis, [(d, (d - 1) % ways) for d in range(ways)])
+            full = lax.dynamic_update_slice_in_dim(
+                full, going_down, (here + far) % ways * step, axis=dim
+            )
+    return full
 
 
 def contract(left, right, left_dim, right_dim):
@@ -40,9 +56,7 @@
         lift_grad = (hidden_grad * gated).astype(jnp.bfloat16)
         return (gate_grad, lift_grad)
 
-    cotangent = lax.all_gather(grad_out.astype(jnp.bfloat16), "tensor", axis=0, tiled=True).astype(
-        grad_out.dtype
-    )
+    cotangent = gather_around(grad_out.astype(jnp.bfloat16), "tensor", 0).astype(grad_out.dtype)
 
     def jacobian(state):
         gate_grad, lift_grad = branch_rows(state.astype(jnp.bfloat16))

time: 304 us -> 335 us (1.10)
  starting transfers between devices: 0.26 us -> 32.5 us
  blocking collectives: 42.6 us -> 20.4 us
  waiting for transfers between devices: 182 us -> 195 us
  matrix products: 54.4 us -> 61.5 us
    ppermute x0 -> x15, starting transfers between devices: none -> 32.2 us  [the longest x7 31.3 us: gather_around(): lax.ppermute(going_down, axis, [(d, (d - 1) % ways) for d in range(ways)])]
    all_gather x1 -> x0, blocking collectives: 24 us -> none  [body(): lax.all_gather(grad_out.astype(jnp.bfloat16), 'tensor', axis=0, tiled=True)]
    ppermute x0 -> x15, waiting for transfers between devices: none -> 14.2 us  [the longest x8 14.1 us: gather_around(): lax.ppermute(going_up, axis, [(d, (d + 1) % ways) for d in range(ways)])]
    dot_general x12, matrix products: 54.4 us -> 61.5 us  [contract(): lax.dot_general(left, right, (((left_dim,), (right_dim,)), ((), ())), pre...]
  transfers between devices with their start and end apart: 2 -> 17, of which waited for: 2 -> 9; matrix products, arithmetic and copies ran while one was open for 0% -> 3% of each run, Pallas kernels for 0% -> 0%
where the time goes in v1:
time: 335 us
  waiting for transfers between devices  195 us (58%)
  matrix products  61.5 us (18%)
  starting transfers between devices  32.5 us (10%)
  blocking collectives  20.4 us (6%)
  between operations  15.9 us (5%)
  other arithmetic  8.27 us (2%)
    psum x2, waiting for transfers between devices, jacobian(): normed_grad = lax.psum(partial_sum, 'tensor')  180 us
    dot_general x12, matrix products, contract(): lax.dot_general(left, right, (((left_dim,), (right_dim,)), ((), ())), pre...  61.5 us
    ppermute x7, starting transfers between devices, gather_around(): lax.ppermute(going_down, axis, [(d, (d - 1) % ways) for d in range(ways)])  31.3 us
    all_gather x1, blocking collectives, body(): z_full = lax.all_gather(z_star, 'tensor', axis=0, tiled=True)  20.4 us
    ppermute x8, waiting for transfers between devices, gather_around(): lax.ppermute(going_up, axis, [(d, (d + 1) % ways) for d in range(ways)])  14.1 us
  transfers between devices with their start and end apart: 17, of which 9 were waited for; matrix products, arithmetic and copies ran while one was open for 3% of the time, Pallas kernels for 0%

profile of v1, /device:TPU:0, one launch (start us, length us, event | category | flops | bytes accessed | tf_op | source)
XLA Modules:
  0.0 334.7 jit_solution(8210203339734861732)
XLA Ops:
  7.2 0.0 all-reduce.3.cloned.1.call-start
  7.2 0.8 constant_dynamic-update-slice_fusion.15
  8.1 0.5 collective-permute-start
  8.6 5.0 %collective-permute-start.1 = (bf16[2,5120]{1,0:T(2,128)(2,1)S(1)}, bf16[2,5120]{1,0:T(2,128)(2,1)S(1)}, u32[]{:S(2)}, u32[]{:S(2)}) collective-permute-start(bf16[2,5120]{1,0:T(2,128)(2,1)S(1)} %get-tuple-element.9), channel_id=1, source_target_pairs={{0,15},{1,0},{2,1},{3,2},{4,3},{5,4},{6,5},{7,6},{8,7},{9,8},{10,9... | collective-permute-start | bytes 61448 | tf_op jit(solution)/shard_map/ppermute | solution.py:16
  13.7 20.4 %all-gather = bf16[16,2,5120]{2,1,0:T(2,128)(2,1)S(1)} all-gather(bf16[1,2,5120]{2,1,0:T(2,128)(2,1)} %bitcast.19), channel_id=1, replica_groups=mesh['group'=2,'tensor'=16] {'tensor'}, dimensions={0}, use_global_device_ids=true | all-gather | bytes 348160 | tf_op jit(solution)/shard_map/all_gather | solution.py:44
  34.1 0.1 reshape.28
  34.2 0.0 copy-start
  34.2 0.2 multiply_reduce_fusion.4
  34.4 1.0 multiply_convert_fusion
  35.4 6.4 %fusion.21 = f32[32,864]{1,0:T(8,128)S(1)} fusion(bf16[32,5120]{1,0:T(8,128)(2,1)S(1)} %multiply_convert_fusion, bf16[5120,864]{0,1:T(8,128)(2,1)} %param.9), kind=kOutput, calls=%fused_computation.60 | convolution fusion | flops 283115520 | bytes 9285632 | tf_op jit(solution)/shard_map/dot_general | solution.py:24
  41.9 2.7 fusion.20
  44.8 0.4 collective-permute-start.2
  45.2 4.1 %collective-permute-start.3 = (bf16[2,5120]{1,0:T(2,128)(2,1)S(1)}, bf16[2,5120]{1,0:T(2,128)(2,1)S(1)}, u32[]{:S(2)}, u32[]{:S(2)}) collective-permute-start(bf16[2,5120]{1,0:T(2,128)(2,1)S(1)} %collective-permute-done.1), channel_id=1, source_target_pairs={{0,15},{1,0},{2,1},{3,2},{4,3},{5,4},{6,5},{7,6},{8,7},{9,8},{10,9... | collective-permute-start | bytes 61448 | tf_op jit(solution)/shard_map/ppermute | solution.py:16
  49.4 1.4 collective-permute-done.2
  50.8 0.0 collective-permute-start.4
  50.8 0.0 collective-permute-done.3
  50.8 4.4 %collective-permute-start.5 = (bf16[2,5120]{1,0:T(2,128)(2,1)S(1)}, bf16[2,5120]{1,0:T(2,128)(2,1)S(1)}, u32[]{:S(2)}, u32[]{:S(2)}) collective-permute-start(bf16[2,5120]{1,0:T(2,128)(2,1)S(1)} %collective-permute-done.3), channel_id=1, source_target_pairs={{0,15},{1,0},{2,1},{3,2},{4,3},{5,4},{6,5},{7,6},{8,7},{9,8},{10,9... | collective-permute-start | bytes 61448 | tf_op jit(solution)/shard_map/ppermute | solution.py:16
  55.3 1.4 collective-permute-done.4
  56.7 0.0 collective-permute-done.5
  56.7 4.4 %collective-permute-start.7 = (bf16[2,5120]{1,0:T(2,128)(2,1)S(1)}, bf16[2,5120]{1,0:T(2,128)(2,1)S(1)}, u32[]{:S(2)}, u32[]{:S(2)}) collective-permute-start(bf16[2,5120]{1,0:T(2,128)(2,1)S(1)} %collective-permute-done.5), channel_id=1, source_target_pairs={{0,15},{1,0},{2,1},{3,2},{4,3},{5,4},{6,5},{7,6},{8,7},{9,8},{10,9... | collective-permute-start | bytes 61448 | tf_op jit(solution)/shard_map/ppermute | solution.py:16
  61.2 1.4 collective-permute-done.6
  62.6 0.0 collective-permute-done.7
  62.6 4.4 %collective-permute-start.9 = (bf16[2,5120]{1,0:T(2,128)(2,1)S(1)}, bf16[2,5120]{1,0:T(2,128)(2,1)S(1)}, u32[]{:S(2)}, u32[]{:S(2)}) collective-permute-start(bf16[2,5120]{1,0:T(2,128)(2,1)S(1)} %collective-permute-done.7), channel_id=1, source_target_pairs={{0,15},{1,0},{2,1},{3,2},{4,3},{5,4},{6,5},{7,6},{8,7},{9,8},{10,9... | collective-permute-start | bytes 61448 | tf_op jit(solution)/shard_map/ppermute | solution.py:16
  67.1 1.4 collective-permute-done.8
  68.5 0.0 collective-permute-done.9
  68.5 4.4 %collective-permute-start.11 = (bf16[2,5120]{1,0:T(2,128)(2,1)S(1)}, bf16[2,5120]{1,0:T(2,128)(2,1)S(1)}, u32[]{:S(2)}, u32[]{:S(2)}) collective-permute-start(bf16[2,5120]{1,0:T(2,128)(2,1)S(1)} %collective-permute-done.9), channel_id=1, source_target_pairs={{0,15},{1,0},{2,1},{3,2},{4,3},{5,4},{6,5},{7,6},{8,7},{9,8},{10,9... | collective-permute-start | bytes 61448 | tf_op jit(solution)/shard_map/ppermute | solution.py:16
  73.0 1.4 collective-permute-done.10
  74.4 0.0 collective-permute-start.12
  74.4 0.0 collective-permute-done.11
  74.4 4.4 %collective-permute-start.13 = (bf16[2,5120]{1,0:T(2,128)(2,1)S(1)}, bf16[2,5120]{1,0:T(2,128)(2,1)S(1)}, u32[]{:S(2)}, u32[]{:S(2)}) collective-permute-start(bf16[2,5120]{1,0:T(2,128)(2,1)S(1)} %collective-permute-done.11), channel_id=1, source_target_pairs={{0,15},{1,0},{2,1},{3,2},{4,3},{5,4},{6,5},{7,6},{8,7},{9,8},{10,9... | collective-permute-start | bytes 61448 | tf_op jit(solution)/shard_map/ppermute | solution.py:16
  78.9 1.4 collective-permute-done.12
  80.3 0.0 collective-permute-start.14
  80.4 5.8 %collective-permute-done.14 = bf16[2,5120]{1,0:T(2,128)(2,1)S(1)} collective-permute-done((bf16[2,5120]{1,0:T(2,128)(2,1)S(1)}, bf16[2,5120]{1,0:T(2,128)(2,1)S(1)}, u32[]{:S(2)}, u32[]{:S(2)}) %collective-permute-start.14) | collective-permute-done | bytes 20512 | tf_op jit(solution)/shard_map/ppermute | solution.py:13
  86.2 0.0 slice-start
  86.2 0.0 slice-start.1
  86.2 6.3 %fusion.19 = f32[32,864]{1,0:T(8,128)S(1)} fusion(bf16[32,5120]{1,0:T(8,128)(2,1)S(1)} %constant_dynamic-update-slice_fusion, bf16[864,5120]{1,0:T(8,128)(2,1)} %param.11), kind=kOutput, calls=%fused_computation.58 | convolution fusion | flops 283115520 | bytes 9285632 | tf_op jit(solution)/shard_map/dot_general | solution.py:24
  92.6 0.0 slice-start.2
  92.6 5.3 %fusion.12 = f32[32,5120]{1,0:T(8,128)S(1)} fusion(bf16[5120,864]{0,1:T(8,128)(2,1)} %param.9, f32[32,864]{1,0:T(8,128)S(1)} %fusion.19, f32[32,864]{1,0:T(8,128)S(1)} %fusion.20, f32[32,864]{1,0:T(8,128)S(1)} %fusion.21), kind=kOutput, calls=%fused_computation.36 | convolution fusion | flops 283392000 | bytes 9834496 | tf_op jit(solution)/shard_map/dot_general | solution.py:24
  97.8 0.0 slice-done.1
  97.9 0.0 copy-start.1
  97.9 0.0 copy-start.2
  97.9 2.5 convolution_add_fusion.1
  100.4 0.0 all-reduce.3.cloned.1.call-update
  100.4 0.2 all-reduce.5.cloned.1.call-start
  100.6 88.9 %all-reduce.3.cloned.1.call-done = f32[32,5120]{1,0:T(8,128)} async-done(((f32[32,5120]{1,0:T(8,128)}), f32[32,5120]{1,0:T(8,128)}) %all-reduce.3.cloned.1.call-update) | async-done | bytes 655376 | tf_op jit(solution)/shard_map/psum | solution.py:64
  189.5 1.3 multiply_reduce_fusion.3
  190.8 1.3 subtract_divide_fusion
  192.1 0.0 slice-start.3
  192.1 0.0 slice-start.4
  192.1 6.3 %fusion.5 = f32[32,864]{1,0:T(8,128)S(1)} fusion(bf16[864,5120]{1,0:T(8,128)(2,1)} %param.11, f32[32,5120]{1,0:T(8,128)S(1)} %subtract_divide_fusion, bf16[32,5120]{1,0:T(8,128)(2,1)S(1)} %constant_dynamic-update-slice_fusion, f32[5120]{0:T(1024)S(1)} %copy-done.2), kind=kOutput, calls=%fused_computation.20 | convolution fusion | flops 283770880 | bytes 9961472 | tf_op jit(solution)/shard_map/dot_general | solution.py:24
  198.4 0.0 slice-start.5
  198.5 5.3 %fusion.13 = f32[32,5120]{1,0:T(8,128)S(1)} fusion(bf16[5120,864]{0,1:T(8,128)(2,1)} %param.9, f32[32,864]{1,0:T(8,128)S(1)} %fusion.5, f32[32,864]{1,0:T(8,128)S(1)} %fusion.20, f32[32,864]{1,0:T(8,128)S(1)} %fusion.21), kind=kOutput, calls=%fused_computation.37 | convolution fusion | flops 283392000 | bytes 9834496 | tf_op jit(solution)/shard_map/dot_general | solution.py:24
  203.7 0.0 slice-done.4
  203.8 2.5 convolution_add_fusion
  206.3 0.0 all-reduce.5.cloned.1.call-update
  206.3 91.6 %all-reduce.5.cloned.1.call-done = f32[32,5120]{1,0:T(8,128)} async-done(((f32[32,5120]{1,0:T(8,128)}), f32[32,5120]{1,0:T(8,128)}) %all-reduce.5.cloned.1.call-update) | async-done | bytes 655376 | tf_op jit(solution)/shard_map/psum | solution.py:64
  297.9 1.3 multiply_reduce_fusion.2
  299.2 2.1 multiply_reduce_fusion
  302.6 0.2 fusion.3
  302.8 0.6 constant_dynamic-slice_fusion
  303.5 6.1 %fusion.9 = f32[32,864]{1,0:T(8,128)S(1)} fusion(bf16[864,5120]{1,0:T(8,128)(2,1)} %param.11, f32[32,5120]{1,0:T(8,128)S(1)} %fusion.3), kind=kOutput, calls=%fused_computation.24 | convolution fusion | flops 283279360 | bytes 9613312 | tf_op jit(solution)/shard_map/dot_general | solution.py:24
  309.6 6.1 %convolution_convert_fusion = bf16[864,5120]{1,0:T(8,128)(2,1)} fusion(f32[32,5120]{1,0:T(8,128)S(1)} %fusion.3, f32[32,864]{1,0:T(8,128)S(1)} %fusion.20, f32[32,864]{1,0:T(8,128)S(1)} %fusion.21), kind=kOutput, calls=%fused_computation | convolution fusion | flops 287868928 | bytes 9723904 | tf_op jit(solution)/shard_map/dot_general | solution.py:24
  315.7 6.1 %convolution_convert_fusion.2 = bf16[5120,864]{0,1:T(8,128)(2,1)} fusion(bf16[32,5120]{1,0:T(8,128)(2,1)S(1)} %multiply_convert_fusion, f32[32,864]{1,0:T(8,128)S(1)} %fusion.9, f32[32,864]{1,0:T(8,128)S(1)} %fusion.20, f32[32,864]{1,0:T(8,128)S(1)} %fusion.21), kind=kOutput, calls=%fused_computation.2 | convolution fusion | flops 287815680 | bytes 9506816 | tf_op jit(solution)/shard_map/dot_general | solution.py:24
  321.8 6.1 %convolution_convert_fusion.1 = bf16[5120,864]{0,1:T(8,128)(2,1)} fusion(bf16[32,5120]{1,0:T(8,128)(2,1)S(1)} %multiply_convert_fusion, f32[32,864]{1,0:T(8,128)S(1)} %fusion.9, f32[32,864]{1,0:T(8,128)S(1)} %fusion.21), kind=kOutput, calls=%fused_computation.1 | convolution fusion | flops 287705088 | bytes 9396224 | tf_op jit(solution)/shard_map/dot_general | solution.py:24
  (34 shorter events, 0.6 us)
Async XLA Ops:
  7.2 182.3 %all-reduce.3.cloned.1.call-start = ((), (), s32[]{:S(2)}) async-start(), calls=%async_computation | async-start | bytes 1310720 | tf_op jit(solution)/shard_map/psum | solution.py:64
  8.1 36.7 %collective-permute-start = (bf16[2,5120]{1,0:T(2,128)(2,1)S(1)}, bf16[2,5120]{1,0:T(2,128)(2,1)S(1)}, u32[]{:S(2)}, u32[]{:S(2)}) collective-permute-start(bf16[2,5120]{1,0:T(2,128)(2,1)S(1)} %get-tuple-element.9), channel_id=1, source_target_pairs={{0,1},{1,2},{2,3},{3,4},{4,5},{5,6},{6,7},{7,8},{8,9},{9,10},{10,1... | collective-permute-start | bytes 61448 | tf_op jit(solution)/shard_map/ppermute | solution.py:13
  8.6 36.6 %collective-permute-start.1 = (bf16[2,5120]{1,0:T(2,128)(2,1)S(1)}, bf16[2,5120]{1,0:T(2,128)(2,1)S(1)}, u32[]{:S(2)}, u32[]{:S(2)}) collective-permute-start(bf16[2,5120]{1,0:T(2,128)(2,1)S(1)} %get-tuple-element.9), channel_id=1, source_target_pairs={{0,15},{1,0},{2,1},{3,2},{4,3},{5,4},{6,5},{7,6},{8,7},{9,8},{10,9... | collective-permute-start | bytes 61448 | tf_op jit(solution)/shard_map/ppermute | solution.py:16
  34.2 7.6 %copy-start = (bf16[5120,864]{0,1:T(8,128)(2,1)S(1)}, bf16[5120,864]{0,1:T(8,128)(2,1)}, u32[]{:S(2)}) copy-start(bf16[5120,864]{0,1:T(8,128)(2,1)} %param.10) | copy-start | bytes 26542084
  44.8 6.0 %collective-permute-start.2 = (bf16[2,5120]{1,0:T(2,128)(2,1)S(1)}, bf16[2,5120]{1,0:T(2,128)(2,1)S(1)}, u32[]{:S(2)}, u32[]{:S(2)}) collective-permute-start(bf16[2,5120]{1,0:T(2,128)(2,1)S(1)} %collective-permute-done), channel_id=1, source_target_pairs={{0,1},{1,2},{2,3},{3,4},{4,5},{5,6},{6,7},{7,8},{8,9},{9,10},{10,1... | collective-permute-start | bytes 61448 | tf_op jit(solution)/shard_map/ppermute | solution.py:13
  45.2 5.6 %collective-permute-start.3 = (bf16[2,5120]{1,0:T(2,128)(2,1)S(1)}, bf16[2,5120]{1,0:T(2,128)(2,1)S(1)}, u32[]{:S(2)}, u32[]{:S(2)}) collective-permute-start(bf16[2,5120]{1,0:T(2,128)(2,1)S(1)} %collective-permute-done.1), channel_id=1, source_target_pairs={{0,15},{1,0},{2,1},{3,2},{4,3},{5,4},{6,5},{7,6},{8,7},{9,8},{10,9... | collective-permute-start | bytes 61448 | tf_op jit(solution)/shard_map/ppermute | solution.py:16
  50.8 5.9 %collective-permute-start.4 = (bf16[2,5120]{1,0:T(2,128)(2,1)S(1)}, bf16[2,5120]{1,0:T(2,128)(2,1)S(1)}, u32[]{:S(2)}, u32[]{:S(2)}) collective-permute-start(bf16[2,5120]{1,0:T(2,128)(2,1)S(1)} %collective-permute-done.2), channel_id=1, source_target_pairs={{0,1},{1,2},{2,3},{3,4},{4,5},{5,6},{6,7},{7,8},{8,9},{9,10},{10,1... | collective-permute-start | bytes 61448 | tf_op jit(solution)/shard_map/ppermute | solution.py:13
  50.8 5.9 %collective-permute-start.5 = (bf16[2,5120]{1,0:T(2,128)(2,1)S(1)}, bf16[2,5120]{1,0:T(2,128)(2,1)S(1)}, u32[]{:S(2)}, u32[]{:S(2)}) collective-permute-start(bf16[2,5120]{1,0:T(2,128)(2,1)S(1)} %collective-permute-done.3), channel_id=1, source_target_pairs={{0,15},{1,0},{2,1},{3,2},{4,3},{5,4},{6,5},{7,6},{8,7},{9,8},{10,9... | collective-permute-start | bytes 61448 | tf_op jit(solution)/shard_map/ppermute | solution.py:16
  56.7 5.9 %collective-permute-start.6 = (bf16[2,5120]{1,0:T(2,128)(2,1)S(1)}, bf16[2,5120]{1,0:T(2,128)(2,1)S(1)}, u32[]{:S(2)}, u32[]{:S(2)}) collective-permute-start(bf16[2,5120]{1,0:T(2,128)(2,1)S(1)} %collective-permute-done.4), channel_id=1, source_target_pairs={{0,1},{1,2},{2,3},{3,4},{4,5},{5,6},{6,7},{7,8},{8,9},{9,10},{10,1... | collective-permute-start | bytes 61448 | tf_op jit(solution)/shard_map/ppermute | solution.py:13
  56.7 5.9 %collective-permute-start.7 = (bf16[2,5120]{1,0:T(2,128)(2,1)S(1)}, bf16[2,5120]{1,0:T(2,128)(2,1)S(1)}, u32[]{:S(2)}, u32[]{:S(2)}) collective-permute-start(bf16[2,5120]{1,0:T(2,128)(2,1)S(1)} %collective-permute-done.5), channel_id=1, source_target_pairs={{0,15},{1,0},{2,1},{3,2},{4,3},{5,4},{6,5},{7,6},{8,7},{9,8},{10,9... | collective-permute-start | bytes 61448 | tf_op jit(solution)/shard_map/ppermute | solution.py:16
  62.6 5.9 %collective-permute-start.8 = (bf16[2,5120]{1,0:T(2,128)(2,1)S(1)}, bf16[2,5120]{1,0:T(2,128)(2,1)S(1)}, u32[]{:S(2)}, u32[]{:S(2)}) collective-permute-start(bf16[2,5120]{1,0:T(2,128)(2,1)S(1)} %collective-permute-done.6), channel_id=1, source_target_pairs={{0,1},{1,2},{2,3},{3,4},{4,5},{5,6},{6,7},{7,8},{8,9},{9,10},{10,1... | collective-permute-start | bytes 61448 | tf_op jit(solution)/shard_map/ppermute | solution.py:13
  62.6 5.9 %collective-permute-start.9 = (bf16[2,5120]{1,0:T(2,128)(2,1)S(1)}, bf16[2,5120]{1,0:T(2,128)(2,1)S(1)}, u32[]{:S(2)}, u32[]{:S(2)}) collective-permute-start(bf16[2,5120]{1,0:T(2,128)(2,1)S(1)} %collective-permute-done.7), channel_id=1, source_target_pairs={{0,15},{1,0},{2,1},{3,2},{4,3},{5,4},{6,5},{7,6},{8,7},{9,8},{10,9... | collective-permute-start | bytes 61448 | tf_op jit(solution)/shard_map/ppermute | solution.py:16
  68.5 5.9 %collective-permute-start.10 = (bf16[2,5120]{1,0:T(2,128)(2,1)S(1)}, bf16[2,5120]{1,0:T(2,128)(2,1)S(1)}, u32[]{:S(2)}, u32[]{:S(2)}) collective-permute-start(bf16[2,5120]{1,0:T(2,128)(2,1)S(1)} %collective-permute-done.8), channel_id=1, source_target_pairs={{0,1},{1,2},{2,3},{3,4},{4,5},{5,6},{6,7},{7,8},{8,9},{9,10},{10,1... | collective-permute-start | bytes 61448 | tf_op jit(solution)/shard_map/ppermute | solution.py:13
  68.5 5.9 %collective-permute-start.11 = (bf16[2,5120]{1,0:T(2,128)(2,1)S(1)}, bf16[2,5120]{1,0:T(2,128)(2,1)S(1)}, u32[]{:S(2)}, u32[]{:S(2)}) collective-permute-start(bf16[2,5120]{1,0:T(2,128)(2,1)S(1)} %collective-permute-done.9), channel_id=1, source_target_pairs={{0,15},{1,0},{2,1},{3,2},{4,3},{5,4},{6,5},{7,6},{8,7},{9,8},{10,9... | collective-permute-start | bytes 61448 | tf_op jit(solution)/shard_map/ppermute | solution.py:16
  74.4 5.9 %collective-permute-start.12 = (bf16[2,5120]{1,0:T(2,128)(2,1)S(1)}, bf16[2,5120]{1,0:T(2,128)(2,1)S(1)}, u32[]{:S(2)}, u32[]{:S(2)}) collective-permute-start(bf16[2,5120]{1,0:T(2,128)(2,1)S(1)} %collective-permute-done.10), channel_id=1, source_target_pairs={{0,1},{1,2},{2,3},{3,4},{4,5},{5,6},{6,7},{7,8},{8,9},{9,10},{10,1... | collective-permute-start | bytes 61448 | tf_op jit(solution)/shard_map/ppermute | solution.py:13
  74.4 5.9 %collective-permute-start.13 = (bf16[2,5120]{1,0:T(2,128)(2,1)S(1)}, bf16[2,5120]{1,0:T(2,128)(2,1)S(1)}, u32[]{:S(2)}, u32[]{:S(2)}) collective-permute-start(bf16[2,5120]{1,0:T(2,128)(2,1)S(1)} %collective-permute-done.11), channel_id=1, source_target_pairs={{0,15},{1,0},{2,1},{3,2},{4,3},{5,4},{6,5},{7,6},{8,7},{9,8},{10,9... | collective-permute-start | bytes 61448 | tf_op jit(solution)/shard_map/ppermute | solution.py:16
  80.3 5.9 %collective-permute-start.14 = (bf16[2,5120]{1,0:T(2,128)(2,1)S(1)}, bf16[2,5120]{1,0:T(2,128)(2,1)S(1)}, u32[]{:S(2)}, u32[]{:S(2)}) collective-permute-start(bf16[2,5120]{1,0:T(2,128)(2,1)S(1)} %collective-permute-done.12), channel_id=1, source_target_pairs={{0,1},{1,2},{2,3},{3,4},{4,5},{5,6},{6,7},{7,8},{8,9},{9,10},{10,1... | collective-permute-start | bytes 61448 | tf_op jit(solution)/shard_map/ppermute | solution.py:13
  86.2 11.6 %slice-start = ((s8[8847360]{0:T(1024)(128)(4,1)}), s8[4194304]{0:T(1024)(128)(4,1)S(1)}, s32[]{:S(2)}) async-start(s8[8847360]{0:T(1024)(128)(4,1)} %bitcast.15), calls=%async_computation.2 | async-start | bytes 8388608
  86.2 11.6 %slice-start.1 = ((s8[8847360]{0:T(1024)(128)(4,1)}), s8[458752]{0:T(1024)(128)(4,1)S(1)}, s32[]{:S(2)}) async-start(s8[8847360]{0:T(1024)(128)(4,1)} %bitcast.15), calls=%async_computation.3 | async-start | bytes 917504
  92.6 5.3 %slice-start.2 = ((s8[8847360]{0:T(1024)(128)(4,1)}), s8[4194304]{0:T(1024)(128)(4,1)S(1)}, s32[]{:S(2)}) async-start(s8[8847360]{0:T(1024)(128)(4,1)} %bitcast.15), calls=%async_computation.4 | async-start | bytes 8388608
  97.9 91.6 %copy-start.1 = (f32[5120]{0:T(1024)S(1)}, f32[5120]{0:T(1024)}, u32[]{:S(2)}) copy-start(f32[5120]{0:T(1024)} %param.12) | copy-start | bytes 61444
  97.9 94.2 %copy-start.2 = (f32[5120]{0:T(1024)S(1)}, f32[5120]{0:T(1024)}, u32[]{:S(2)}) copy-start(f32[5120]{0:T(1024)} %param.13) | copy-start | bytes 61444
  100.4 197.5 %all-reduce.5.cloned.1.call-start = ((), (), s32[]{:S(2)}) async-start(), calls=%async_computation.1 | async-start | bytes 1310720 | tf_op jit(solution)/shard_map/psum | solution.py:64
  192.1 11.6 %slice-start.3 = ((s8[8847360]{0:T(1024)(128)(4,1)}), s8[4194304]{0:T(1024)(128)(4,1)S(1)}, s32[]{:S(2)}) async-start(s8[8847360]{0:T(1024)(128)(4,1)} %bitcast.17), calls=%async_computation.5 | async-start | bytes 8388608
  192.1 11.6 %slice-start.4 = ((s8[8847360]{0:T(1024)(128)(4,1)}), s8[458752]{0:T(1024)(128)(4,1)S(1)}, s32[]{:S(2)}) async-start(s8[8847360]{0:T(1024)(128)(4,1)} %bitcast.17), calls=%async_computation.6 | async-start | bytes 917504
  198.4 5.3 %slice-start.5 = ((s8[8847360]{0:T(1024)(128)(4,1)}), s8[4194304]{0:T(1024)(128)(4,1)S(1)}, s32[]{:S(2)}) async-start(s8[8847360]{0:T(1024)(128)(4,1)} %bitcast.17), calls=%async_computation.7 | async-start | bytes 8388608
Sparse Core Ops, SparseCore 0:
  100.5 88.9 all-reduce.2
  206.4 91.4 all-reduce.4
